TPU v7x, 512 devices: a whole 4x4x16 slice. The times are simulated.
512 devices in a mesh: grp: 8 (over y_lo, x), shard: 64 (over z, y_hi, core).
Axes of the slice: x: 4, y: 4 (y_hi: 2, y_lo: 2; y = y_hi * 2 + y_lo), z: 16, core: 2. Of those that a mesh axis runs over, the one named last changes fastest.
Arguments:
- window: bfloat16 [128, 4096], P('grp'), may hold values from -6 to 6
- weight: bfloat16 [11008, 4096], P('shard'), may hold values from -0.09375 to 0.09375
- factor_a: bfloat16 [1024, 4, 4096], P(('grp', 'shard')), may hold values from -6 to 6
- factor_b: bfloat16 [1024, 4, 11008], P(('grp', 'shard')), may hold values from -6 to 6
- fitness: float32 [1024], P(('grp', 'shard')), may hold values from -4 to 4
Outputs:
- perturbed: bfloat16 [11008, 16384], P('shard', 'grp')
- update: float32 [11008, 4096], P('shard', 'grp')
All inputs are finite; a program needn't handle non-finite values.
Results may differ from a plain program's by a relative error of at most 0.0029.
Values may be sent and summed in bfloat16 or wider, within the bound.
A program may use at most 64 MiB of HBM per device.

v0:
```python
import math
import jax
import jax.numpy as jnp
from jax import lax
from jax.sharding import Mesh
from jax.sharding import PartitionSpec as P

SHARD = ("shard_0", "shard_1", "shard_2")
GRP_SHARD = ("grp", "shard_0", "shard_1", "shard_2")


def side_by_side(arrays, axis, dim, along):
    columns = [a.reshape(*a.shape[:along], -1) for a in arrays]
    both = jnp.concatenate(columns, axis=along)
    filled, at, done = (lax.all_gather(both, axis, axis=dim, tiled=True), 0, [])
    for a, column in zip(arrays, columns):
        share = filled[..., at : at + column.shape[along]]
        done.append(share.reshape(*share.shape[:along], *a.shape[along:]))
        at += column.shape[along]
    return tuple(done)


def from_everyone(value, axis):
    peers = lax.axis_size(axis)
    return lax.all_to_all(
        jnp.broadcast_to(value[None], (peers, *value.shape)), axis, 0, 0, tiled=True
    )


def in_order(blocks, dim):
    blocks = jnp.moveaxis(blocks, 0, dim)
    dims = blocks.shape
    return blocks.reshape(*dims[:dim], dims[dim] * dims[dim + 1], *dims[dim + 2 :])


def gathered_copies(value, axis, dim):
    blocks = from_everyone(value, axis)
    return in_order(blocks, dim)


def stacked_from(value, axes, sequence):
    blocks = value[None]
    for k in sequence:
        blocks = lax.all_gather(blocks, axes[k], axis=0, tiled=True)
    block = [lax.axis_size(axes[k]) for k in reversed(sequence)]
    blocks = blocks.reshape(*block, *value.shape)
    turned = sorted(range(len(sequence)), key=lambda place: sequence[len(sequence) - 1 - place])
    return blocks.transpose(*turned, *range(len(sequence), blocks.ndim)).reshape(-1, *value.shape)


def gather_axes(value, axes, sequence, dim):
    return in_order(stacked_from(value, axes, sequence), dim)


def contract(left_rows, right_rows):
    return lax.dot_general(
        left_rows, right_rows, (((0,), (0,)), ((), ())), preferred_element_type=jnp.float32
    )


def local(window, weight, factor_a, factor_b, fitness):
    model_width = window.shape[1]
    cand_dev, factor_rank, _ = factor_a.shape
    shard_count = lax.axis_size(SHARD)
    total_cands = cand_dev * lax.axis_size("grp") * shard_count
    perturb = 0.25 / math.sqrt(model_width)
    step_scale = 0.5 / math.sqrt(total_cands)
    base_out = lax.dot_general(
        weight, window, (((1,), (1,)), ((), ())), preferred_element_type=jnp.float32
    )
    projected = jnp.einsum("td,crd->crt", window, factor_a, preferred_element_type=jnp.float32)
    projected_all, fitness_all = side_by_side((projected, fitness), SHARD, 0, 1)
    columns = lax.all_to_all(factor_b, SHARD, split_axis=2, concat_axis=0, tiled=True)
    col_width = columns.shape[2]
    low_rank = jnp.einsum(
        "crt,crf->fct", projected_all, columns.astype(jnp.float32), precision=lax.Precision.HIGHEST
    )
    perturbed = (
        (base_out[:, None, :] + perturb * low_rank).astype(jnp.bfloat16).reshape(col_width, -1)
    )
    weighted = (fitness_all[:, None, None] * columns.astype(jnp.float32)).astype(jnp.bfloat16)
    exchanged = lax.all_to_all(factor_a, "grp", split_axis=2, concat_axis=0, tiled=True)
    weighted_four = weighted.reshape(shard_count, cand_dev, factor_rank, col_width)
    weighted_flat = gathered_copies(weighted_four, "grp", 1).reshape(-1, col_width)
    owned_width = exchanged.shape[2]
    block_width = owned_width // 4
    update_parts = []
    for part_index in range(4):
        factor_slab = exchanged[:, :, part_index * block_width : (part_index + 1) * block_width]
        gathered = gather_axes(factor_slab, SHARD, (1, 0, 2), 0)
        update_parts.append(contract(weighted_flat, gathered.reshape(-1, block_width)))
    update = jnp.concatenate(update_parts, 1) * step_scale
    return (perturbed, update)


def solution(mesh):
    split = Mesh(
        mesh.devices.reshape(mesh.shape["grp"], 16, 2, 2), ("grp", "shard_0", "shard_1", "shard_2")
    )
    return jax.shard_map(
        local,
        mesh=split,
        in_specs=(
            P("grp", None),
            P(SHARD, None),
            P(GRP_SHARD, None, None),
            P(GRP_SHARD, None, None),
            P(GRP_SHARD),
        ),
        out_specs=(P(SHARD, "grp"), P(SHARD, "grp")),
        check_vma=False,
    )
```

profile of v0, /device:TPU:2, one launch (start us, length us, event | category | flops | bytes accessed | tf_op | source)
XLA Modules:
  0.0 370.6 jit_solution(10360211323301085646)
XLA Ops:
  7.2 0.0 copy-start
  7.2 0.0 all-gather.10.cloned.1.call-start
  7.2 4.5 %copy.56 = bf16[2,4,4096]{1,0,2:T(2,128)(2,1)S(1)} copy(bf16[2,4,4096]{2,1,0:T(4,128)(2,1)} %param.7) | data formatting | bytes 131072 | tf_op args[2]
  11.7 4.6 %reshape.55 = bf16[8,2,2048]{2,1,0:T(2,128)(2,1)} reshape(bf16[4096,2,4]{2,1,0:T(2,128)(2,1)S(1)} %bitcast.65) | data formatting | bytes 131072
  16.3 14.9 %all_to_all.41 = bf16[8,2,2048]{2,1,0:T(2,128)(2,1)} all-to-all(bf16[8,2,2048]{2,1,0:T(2,128)(2,1)} %reshape.55), channel_id=1, replica_groups=mesh['grp'=8,'shard_0'=16,'shard_1'=2,'shard_2'=2] {'grp'}, dimensions={0} | all-to-all | bytes 131072 | tf_op jit(solution)/shard_map/all_to_all | solution.py:82
  31.2 5.3 %reshape.56 = bf16[4096,2,4]{2,1,0:T(2,128)(2,1)S(1)} reshape(bf16[8,2,2048]{2,1,0:T(2,128)(2,1)} %all_to_all.41) | data formatting | bytes 131072
  36.5 3.3 copy.57
  39.8 0.8 fusion.3
  40.6 5.9 %all-gather = bf16[32,4,128]{2,1,0:T(4,128)(2,1)S(1)} all-gather(bf16[16,4,128]{2,1,0:T(4,128)(2,1)S(1)} %get-tuple-element.12), channel_id=2, replica_groups=mesh['grp'=8,'shard_0'=16,'shard_1'=2,'shard_2'=2] {'shard_1'}, dimensions={0}, use_global_device_ids=true | all-gather | bytes 49152 | tf_op jit(solution)/shard_map/all_gather | solution.py:44
  46.5 36.9 %all_gather.41 = bf16[32,16,4,128]{3,1,2,0:T(8,128)(2,1)} all-gather(bf16[2,16,4,128]{3,1,2,0:T(8,128)(2,1)S(1)} %copy.58), channel_id=1, replica_groups=mesh['grp'=8,'shard_0'=16,'shard_1'=2,'shard_2'=2] {'shard_0'}, dimensions={0}, use_global_device_ids=true | all-gather | bytes 557056 | tf_op jit(solution)/shard_map/all_gather | solution.py:44
  83.4 0.0 all-gather.10.cloned.1.call-update
  83.4 0.0 all-gather.12.cloned.1.call-start
  83.5 5.9 %all-gather.1 = bf16[32,4,128]{2,1,0:T(4,128)(2,1)S(1)} all-gather(bf16[16,4,128]{2,1,0:T(4,128)(2,1)S(1)} %get-tuple-element.15), channel_id=3, replica_groups=mesh['grp'=8,'shard_0'=16,'shard_1'=2,'shard_2'=2] {'shard_1'}, dimensions={0}, use_global_device_ids=true | all-gather | bytes 49152 | tf_op jit(solution)/shard_map/all_gather | solution.py:44
  89.4 31.2 %all_gather.44 = bf16[32,16,4,128]{3,1,2,0:T(8,128)(2,1)} all-gather(bf16[2,16,4,128]{3,1,2,0:T(8,128)(2,1)S(1)} %copy.60), channel_id=1, replica_groups=mesh['grp'=8,'shard_0'=16,'shard_1'=2,'shard_2'=2] {'shard_0'}, dimensions={0}, use_global_device_ids=true | all-gather | bytes 557056 | tf_op jit(solution)/shard_map/all_gather | solution.py:44
  120.6 0.0 all-gather.12.cloned.1.call-update
  120.6 0.0 copy-done.6
  120.7 9.1 %copy.52 = bf16[2,4,11008]{1,0,2:T(2,128)(2,1)} copy(bf16[2,4,11008]{2,1,0:T(4,128)(2,1)S(1)} %copy-done.6) | data formatting | bytes 352256 | tf_op args[3]
  129.8 11.3 %reshape.53 = bf16[64,2,688]{2,1,0:T(2,128)(2,1)} reshape(bf16[11008,2,4]{2,1,0:T(2,128)(2,1)} %bitcast.62) | data formatting | bytes 352256
  141.0 11.0 %all-to-all-start = ((bf16[64,2,688]{2,1,0:T(2,128)(2,1)}), bf16[64,2,688]{2,1,0:T(2,128)(2,1)S(1)}, u32[]{:S(2)}, u32[]{:S(2)}) async-start(bf16[64,2,688]{2,1,0:T(2,128)(2,1)} %reshape.53), calls=%async_computation | async-start | bytes 393216 | tf_op jit(solution)/shard_map/all_to_all | solution.py:73
  152.0 0.0 all-gather.14.cloned.1.call-start
  152.1 5.9 %all-gather.2 = bf16[32,4,128]{2,1,0:T(4,128)(2,1)S(1)} all-gather(bf16[16,4,128]{2,1,0:T(4,128)(2,1)S(1)} %get-tuple-element.14), channel_id=4, replica_groups=mesh['grp'=8,'shard_0'=16,'shard_1'=2,'shard_2'=2] {'shard_1'}, dimensions={0}, use_global_device_ids=true | all-gather | bytes 49152 | tf_op jit(solution)/shard_map/all_gather | solution.py:44
  158.0 34.8 %all_gather.47 = bf16[32,16,4,128]{3,1,2,0:T(8,128)(2,1)} all-gather(bf16[2,16,4,128]{3,1,2,0:T(8,128)(2,1)S(1)} %copy.62), channel_id=1, replica_groups=mesh['grp'=8,'shard_0'=16,'shard_1'=2,'shard_2'=2] {'shard_0'}, dimensions={0}, use_global_device_ids=true | all-gather | bytes 557056 | tf_op jit(solution)/shard_map/all_gather | solution.py:44
  192.8 0.0 all-gather.14.cloned.1.call-update
  192.9 0.0 copy-done.7
  192.9 0.2 fusion.1
  193.1 0.1 reshape.37
  193.2 0.0 copy-done.9
  193.2 0.1 copy.50
  193.3 0.1 maximum_bitcast_fusion
  193.4 75.5 %all-gather.4 = f32[64,2,65]{2,1,0:T(2,128)S(1)} all-gather(f32[1,2,65]{2,1,0:T(2,128)S(1)} %maximum_bitcast_fusion), channel_id=1, replica_groups=mesh['grp'=8,'shard_0'=16,'shard_1'=2,'shard_2'=2] {'shard_0','shard_1',..., dimensions={0}, use_global_device_ids=true | all-gather | bytes 33800 | tf_op jit(solution)/shard_map/all_gather | solution.py:15
  268.9 0.6 copy-done.5
  269.5 0.2 slice_reduce_fusion
  269.7 0.1 mul.30
  269.8 5.9 %all-gather.3 = bf16[32,4,128]{2,1,0:T(4,128)(2,1)S(1)} all-gather(bf16[16,4,128]{2,1,0:T(4,128)(2,1)S(1)} %get-tuple-element.13), channel_id=5, replica_groups=mesh['grp'=8,'shard_0'=16,'shard_1'=2,'shard_2'=2] {'shard_1'}, dimensions={0}, use_global_device_ids=true | all-gather | bytes 49152 | tf_op jit(solution)/shard_map/all_gather | solution.py:44
  275.7 0.6 copy.64
  276.3 0.0 all-to-all-done
  276.3 6.3 %reshape.54 = bf16[11008,2,4]{2,1,0:T(2,128)(2,1)} reshape(bf16[64,2,688]{2,1,0:T(2,128)(2,1)S(1)} %all-to-all-done) | data formatting | bytes 352256
  282.6 10.4 %copy.53 = bf16[2,4,64,172]{3,1,0,2:T(4,128)(2,1)S(1)} copy(bf16[2,4,64,172]{1,0,3,2:T(2,128)(2,1)} %bitcast.61) | data formatting | bytes 352256 | tf_op jit(solution)/shard_map/all_to_all | solution.py:73
  293.0 0.0 copy-start.4
  293.0 0.2 multiply_convert_fusion
  293.2 1.9 broadcast_in_dim.18
  295.1 4.8 %all-to-all-start.1 = ((bf16[8,64,2,4,172]{4,3,2,1,0:T(4,128)(2,1)}), bf16[8,64,2,4,172]{4,3,2,1,0:T(4,128)(2,1)S(1)}, u32[]{:S(2)}, u32[]{:S(2)}) async-start(bf16[8,64,2,4,172]{4,3,2,1,0:T(4,128)(2,1)} %broadcast_in_dim.18), calls=%async_computation.1 | async-start | bytes 4194304 | tf_op jit(solution)/shard_map/all_to_all | solution.py:25
  299.9 31.9 %all_gather.50 = bf16[32,16,4,128]{3,1,2,0:T(8,128)(2,1)} all-gather(bf16[2,16,4,128]{3,1,2,0:T(8,128)(2,1)} %copy.64), channel_id=1, replica_groups=mesh['grp'=8,'shard_0'=16,'shard_1'=2,'shard_2'=2] {'shard_0'}, dimensions={0}, use_global_device_ids=true | all-gather | bytes 557056 | tf_op jit(solution)/shard_map/all_gather | solution.py:44
  331.8 0.0 all-gather.16.cloned.1.call-update
  331.8 1.5 copy.51
  333.3 1.6 copy.54
  334.9 1.4 fusion.4
  336.3 3.1 fusion
  339.4 2.2 copy.66
  341.6 2.8 copy.59
  344.4 2.8 copy.61
  347.2 2.8 copy.63
  350.0 2.8 copy.65
  352.8 0.0 all-to-all-done.1
  352.8 2.5 copy.55
  355.3 3.1 reshape_reshape.3
  358.4 0.0 copy-start.1
  358.4 2.1 fusion.5
  360.5 0.8 fusion.6
  361.3 0.4 copy-done.2
  361.7 0.8 fusion.7
  362.5 0.1 copy-done.3
  362.6 0.8 fusion.8
  363.3 0.8 maximum_multiply_fusion
  (19 shorter events, 0.0 us)
Async XLA Ops:
  7.2 327.8 %copy-start = (bf16[172,4096]{1,0:T(8,128)(2,1)S(1)}, bf16[172,4096]{1,0:T(8,128)(2,1)}, u32[]{:S(2)}) copy-start(bf16[172,4096]{1,0:T(8,128)(2,1)} %param.6) | copy-start | bytes 4227076
  7.2 334.4 %all-gather.10.cloned.1.call-start = ((), (), s32[]{:S(2)}) async-start(), calls=%async_computation.3 | async-start | bytes 1572864 | tf_op jit(solution)/shard_map/all_gather | solution.py:44
  39.8 80.9 %copy-start.6 = (bf16[2,4,11008]{2,1,0:T(4,128)(2,1)S(1)}, bf16[2,4,11008]{2,1,0:T(4,128)(2,1)}, u32[]{:S(2)}) copy-start(bf16[2,4,11008]{2,1,0:T(4,128)(2,1)} %param.8) | copy-start | bytes 528388
  83.4 260.9 %all-gather.12.cloned.1.call-start = ((), (), s32[]{:S(2)}) async-start(), calls=%async_computation.4 | async-start | bytes 1572864 | tf_op jit(solution)/shard_map/all_gather | solution.py:44
  129.8 63.1 %copy-start.7 = (bf16[16,4096]{1,0:T(8,128)(2,1)S(1)}, bf16[16,4096]{1,0:T(8,128)(2,1)}, u32[]{:S(2)}) copy-start(bf16[16,4096]{1,0:T(8,128)(2,1)} %param.5) | copy-start | bytes 393220
  129.8 63.1 %copy-start.8 = (bf16[2,4,4096]{2,1,0:T(4,128)(2,1)S(1)}, bf16[2,4,4096]{2,1,0:T(4,128)(2,1)}, u32[]{:S(2)}) copy-start(bf16[2,4,4096]{2,1,0:T(4,128)(2,1)} %param.7) | copy-start | bytes 196612
  129.8 63.4 %copy-start.9 = (f32[2]{0:T(128)S(1)}, f32[2]{0:T(128)}, u32[]{:S(2)}) copy-start(f32[2]{0:T(128)} %param.9) | copy-start | bytes 28
  141.0 135.3 %all-to-all-start = ((bf16[64,2,688]{2,1,0:T(2,128)(2,1)}), bf16[64,2,688]{2,1,0:T(2,128)(2,1)S(1)}, u32[]{:S(2)}, u32[]{:S(2)}) async-start(bf16[64,2,688]{2,1,0:T(2,128)(2,1)} %reshape.53), calls=%async_computation | async-start | bytes 393216 | tf_op jit(solution)/shard_map/all_to_all | solution.py:73
  152.0 195.2 %all-gather.14.cloned.1.call-start = ((), (), s32[]{:S(2)}) async-start(), calls=%async_computation.5 | async-start | bytes 1572864 | tf_op jit(solution)/shard_map/all_gather | solution.py:44
  268.9 0.6 copy-start.5
  293.0 2.1 copy-start.4
  295.1 57.7 %all-to-all-start.1 = ((bf16[8,64,2,4,172]{4,3,2,1,0:T(4,128)(2,1)}), bf16[8,64,2,4,172]{4,3,2,1,0:T(4,128)(2,1)S(1)}, u32[]{:S(2)}, u32[]{:S(2)}) async-start(bf16[8,64,2,4,172]{4,3,2,1,0:T(4,128)(2,1)} %broadcast_in_dim.18), calls=%async_computation.1 | async-start | bytes 4194304 | tf_op jit(solution)/shard_map/all_to_all | solution.py:25
  299.9 50.1 %all-gather.16.cloned.1.call-start = ((), (), s32[]{:S(2)}) async-start(), calls=%async_computation.6 | async-start | bytes 1572864 | tf_op jit(solution)/shard_map/all_gather | solution.py:44
  358.4 2.1 copy-start.1
  360.5 1.2 copy-start.2
  361.3 1.3 copy-start.3
Sparse Core Ops, SparseCore 0:
  83.6 14.1 all-gather.9
  120.8 15.1 all-gather.11
  193.0 17.0 all-gather.13
  331.9 15.6 all-gather.15
where the time goes:
time: 372 us; the launch traced here: 371 us
  blocking collectives  249 us (67%)
  local copies, waits for them, and re-layouts  81.7 us (22%)
  starting transfers between devices  15.9 us (4%)
  between operations  13.9 us (4%)
  matrix products  9.06 us (2%)
    all_gather x8, blocking collectives, stacked_from(): blocks = lax.all_gather(blocks, axes[k], axis=0, tiled=True)  159 us
    all_gather x1, blocking collectives, side_by_side(): filled, at, done = (lax.all_gather(both, axis, axis=dim, tiled=True), 0, [])  75.5 us
    unnamed x27, local copies, waits for them, and re-layouts  44.3 us
    all_to_all x1, blocking collectives, local(): lax.all_to_all(factor_a, 'grp', split_axis=2, concat_axis=0, tiled=True)  14.9 us
    transpose x4, local copies, waits for them, and re-layouts, stacked_from(): blocks.transpose(*turned, *range(len(sequence), blocks.ndim))  11.1 us
    all_to_all x1, starting transfers between devices, local(): lax.all_to_all(factor_b, SHARD, split_axis=2, concat_axis=0, tiled=True)  11 us
    all_to_all x1, local copies, waits for them, and re-layouts, local(): lax.all_to_all(factor_b, SHARD, split_axis=2, concat_axis=0, tiled=True)  10.4 us
  transfers between devices with their start and end apart: 6, of which 0 were waited for; matrix products, arithmetic and copies ran while one was open for 17% of the time, Pallas kernels for 0%

commit v1 on v0

--- a/solution.py
+++ b/solution.py
@@ -41,7 +41,9 @@
 def stacked_from(value, axes, sequence):
     blocks = value[None]
     for k in sequence:
-        blocks = lax.all_gather(blocks, axes[k], axis=0, tiled=True)
+        blocks = jnp.concatenate(
+            lax.all_to_all(jnp.stack([blocks] * lax.axis_size(axes[k])), axes[k], 0, 0), axis=0
+        )
     block = [lax.axis_size(axes[k]) for k in reversed(sequence)]
     blocks = blocks.reshape(*block, *value.shape)
     turned = sorted(range(len(sequence)), key=lambda place: sequence[len(sequence) - 1 - place])

time: 372 us -> 419 us (1.13)
  the two profiles are of different devices: /device:TPU:2 before, /device:TPU:39 now
where the time goes in v1:
time: 419 us; the launch traced here: 416 us
  blocking collectives  234 us (56%)
  local copies, waits for them, and re-layouts  77.1 us (18%)
  starting transfers between devices  44.4 us (11%)
  waiting for transfers between devices  36.7 us (9%)
  other arithmetic  13 us (3%)
  matrix products  9.74 us (2%)
    all_to_all x6, blocking collectives, stacked_from(): lax.all_to_all(jnp.stack([blocks] * lax.axis_size(axes[k])), axes[k], 0, 0)  92.1 us
    all_gather x1, blocking collectives, side_by_side(): filled, at, done = (lax.all_gather(both, axis, axis=dim, tiled=True), 0, [])  88.8 us
    unnamed x41, local copies, waits for them, and re-layouts  45.2 us
    all_to_all x1, blocking collectives, local(): lax.all_to_all(factor_b, SHARD, split_axis=2, concat_axis=0, tiled=True)  44.3 us
    all_to_all x6, starting transfers between devices, stacked_from(): lax.all_to_all(jnp.stack([blocks] * lax.axis_size(axes[k])), axes[k], 0, 0)  39.2 us
    all_to_all x1, waiting for transfers between devices, from_everyone(): lax.all_to_all(jnp.broadcast_to(value[None], (peers, *value.shape)), axis...  22.9 us
    all_to_all x6, waiting for transfers between devices, stacked_from(): lax.all_to_all(jnp.stack([blocks] * lax.axis_size(axes[k])), axes[k], 0, 0)  13.8 us
    another operation x8, other arithmetic, stacked_from(): jnp.stack([blocks] * lax.axis_size(axes[k]))  12 us
  transfers between devices with their start and end apart: 7, of which 5 were waited for; matrix products, arithmetic and copies ran while one was open for 17% of the time, Pallas kernels for 0%

profile of v1, /device:TPU:39, one launch (start us, length us, event | category | flops | bytes accessed | tf_op | source)
XLA Modules:
  0.0 415.9 jit_solution(3959636218383301764)
XLA Ops:
  0.6 4.5 %copy.37 = bf16[2,4,4096]{1,0,2:T(2,128)(2,1)S(1)} copy(bf16[2,4,4096]{2,1,0:T(4,128)(2,1)} %param.7) | data formatting | bytes 131072 | tf_op args[2]
  5.1 4.6 %reshape.43 = bf16[8,2,2048]{2,1,0:T(2,128)(2,1)} reshape(bf16[4096,2,4]{2,1,0:T(2,128)(2,1)S(1)} %bitcast.77) | data formatting | bytes 131072
  9.7 8.8 %all_to_all.101 = bf16[8,2,2048]{2,1,0:T(2,128)(2,1)} all-to-all(bf16[8,2,2048]{2,1,0:T(2,128)(2,1)} %reshape.43), channel_id=1, replica_groups=mesh['grp'=8,'shard_0'=16,'shard_1'=2,'shard_2'=2] {'grp'}, dimensions={0} | all-to-all | bytes 131072 | tf_op jit(solution)/shard_map/all_to_all | solution.py:84
  18.6 5.3 %reshape.44 = bf16[4096,2,4]{2,1,0:T(2,128)(2,1)S(1)} reshape(bf16[8,2,2048]{2,1,0:T(2,128)(2,1)} %all_to_all.101) | data formatting | bytes 131072
  23.8 3.3 copy.38
  27.1 0.8 slice_bitcast_fusion.3
  27.9 0.6 pad_maximum_fusion.4
  28.6 3.9 all-to-all-start.3
  32.4 0.6 pad_maximum_fusion.5
  33.1 3.7 all-to-all-done.3
  36.7 3.3 all-to-all-start.6
  40.0 0.6 pad_maximum_fusion.6
  40.6 3.7 all-to-all-done.6
  44.3 3.3 all-to-all-start.9
  47.6 0.6 pad_maximum_fusion.7
  48.2 3.7 all-to-all-done.9
  51.8 3.3 all-to-all-start.12
  55.1 11.0 %copy.33 = bf16[2,4,11008]{1,0,2:T(2,128)(2,1)} copy(bf16[2,4,11008]{2,1,0:T(4,128)(2,1)} %param.8) | data formatting | bytes 352256 | tf_op args[3]
  66.1 10.6 %reshape.41 = bf16[64,2,688]{2,1,0:T(2,128)(2,1)S(1)} reshape(bf16[11008,2,4]{2,1,0:T(2,128)(2,1)} %bitcast.74) | data formatting | bytes 352256
  76.7 44.3 %all_to_all.102 = bf16[64,2,688]{2,1,0:T(2,128)(2,1)S(1)} all-to-all(bf16[64,2,688]{2,1,0:T(2,128)(2,1)S(1)} %reshape.41), channel_id=1, replica_groups=mesh['grp'=8,'shard_0'=16,'shard_1'=2,'shard_2'=2] {'shard_0','shard_1',..., dimensions={0} | all-to-all | bytes 352256 | tf_op jit(solution)/shard_map/all_to_all | solution.py:75
  121.0 0.2 stack.37
  121.3 31.2 %all_to_all.103 = bf16[16,2,16,4,128]{4,3,2,1,0:T(4,128)(2,1)} all-to-all(bf16[16,2,16,4,128]{4,3,2,1,0:T(4,128)(2,1)S(1)} %stack.37), channel_id=1, replica_groups=mesh['grp'=8,'shard_0'=16,'shard_1'=2,'shard_2'=2] {'shard_0'}, dimensions={0} | all-to-all | bytes 1048576 | tf_op jit(solution)/shard_map/all_to_all | solution.py:45
  152.5 0.2 stack.40
  152.7 33.7 %all_to_all.104 = bf16[16,2,16,4,128]{4,3,2,1,0:T(4,128)(2,1)} all-to-all(bf16[16,2,16,4,128]{4,3,2,1,0:T(4,128)(2,1)S(1)} %stack.40), channel_id=1, replica_groups=mesh['grp'=8,'shard_0'=16,'shard_1'=2,'shard_2'=2] {'shard_0'}, dimensions={0} | all-to-all | bytes 1048576 | tf_op jit(solution)/shard_map/all_to_all | solution.py:45
  186.4 1.0 stack.43
  187.5 10.2 %all-to-all-start.10 = ((bf16[16,2,16,4,128]{4,3,2,1,0:T(4,128)(2,1)}), bf16[16,2,16,4,128]{4,3,2,1,0:T(4,128)(2,1)S(1)}, u32[]{:S(2)}, u32[]{:S(2)}) async-start(bf16[16,2,16,4,128]{4,3,2,1,0:T(4,128)(2,1)} %stack.43), calls=%async_computation.10 | async-start | bytes 1048576 | tf_op jit(solution)/shard_map/all_to_all | solution.py:45
  197.7 0.2 fusion.1
  198.2 88.8 %all-gather = f32[64,2,65]{2,1,0:T(2,128)S(1)} all-gather(f32[1,2,65]{2,1,0:T(2,128)S(1)} %maximum_bitcast_fusion), channel_id=1, replica_groups=mesh['grp'=8,'shard_0'=16,'shard_1'=2,'shard_2'=2] {'shard_0','shard_1',..., dimensions={0}, use_global_device_ids=true | all-gather | bytes 33800 | tf_op jit(solution)/shard_map/all_gather | solution.py:15
  287.0 0.6 copy-done.8
  287.6 0.2 slice_reduce_fusion
  287.8 0.1 mul.30
  287.9 6.3 %reshape.42 = bf16[11008,2,4]{2,1,0:T(2,128)(2,1)} reshape(bf16[64,2,688]{2,1,0:T(2,128)(2,1)S(1)} %all_to_all.102) | data formatting | bytes 352256
  294.2 10.4 %copy.34 = bf16[2,4,64,172]{3,1,0,2:T(4,128)(2,1)S(1)} copy(bf16[2,4,64,172]{1,0,3,2:T(2,128)(2,1)} %bitcast.73) | data formatting | bytes 352256 | tf_op jit(solution)/shard_map/all_to_all | solution.py:75
  304.6 0.2 multiply_convert_fusion
  304.8 1.9 broadcast_in_dim.2
  306.7 5.2 %all-to-all-start.1 = ((bf16[8,64,2,4,172]{4,3,2,1,0:T(4,128)(2,1)}), bf16[8,64,2,4,172]{4,3,2,1,0:T(4,128)(2,1)S(1)}, u32[]{:S(2)}, u32[]{:S(2)}) async-start(bf16[8,64,2,4,172]{4,3,2,1,0:T(4,128)(2,1)} %broadcast_in_dim.2), calls=%async_computation.1 | async-start | bytes 4194304 | tf_op jit(solution)/shard_map/all_to_all | solution.py:25
  311.9 3.0 pad_maximum_fusion
  314.9 3.0 pad_maximum_fusion.1
  317.9 1.5 pad_maximum_fusion.2
  319.4 22.9 %all-to-all-done.1 = bf16[8,64,2,4,172]{4,3,2,1,0:T(4,128)(2,1)S(1)} async-done(((bf16[8,64,2,4,172]{4,3,2,1,0:T(4,128)(2,1)}), bf16[8,64,2,4,172]{4,3,2,1,0:T(4,128)(2,1)S(1)}, u32[]{:S(2)}, u32[]{:S(2)}) %all-to-all-start.1) | async-done | bytes 1409056 | tf_op jit(solution)/shard_map/all_to_all | solution.py:25
  342.2 7.4 %all_to_all.105 = bf16[2,32,16,4,128]{4,3,2,1,0:T(4,128)(2,1)} all-to-all(bf16[2,32,16,4,128]{4,3,2,1,0:T(4,128)(2,1)} %pad_maximum_fusion), channel_id=1, replica_groups=mesh['grp'=8,'shard_0'=16,'shard_1'=2,'shard_2'=2] {'shard_2'}, dimensions={0} | all-to-all | bytes 2097152 | tf_op jit(solution)/shard_map/all_to_all | solution.py:45
  349.7 5.5 %all_to_all.106 = bf16[2,32,16,4,128]{4,3,2,1,0:T(4,128)(2,1)} all-to-all(bf16[2,32,16,4,128]{4,3,2,1,0:T(4,128)(2,1)S(1)} %copy-done.3), channel_id=1, replica_groups=mesh['grp'=8,'shard_0'=16,'shard_1'=2,'shard_2'=2] {'shard_2'}, dimensions={0} | all-to-all | bytes 2097152 | tf_op jit(solution)/shard_map/all_to_all | solution.py:45
  355.2 5.4 %all_to_all.107 = bf16[2,32,16,4,128]{4,3,2,1,0:T(4,128)(2,1)} all-to-all(bf16[2,32,16,4,128]{4,3,2,1,0:T(4,128)(2,1)S(1)} %copy-done.4), channel_id=1, replica_groups=mesh['grp'=8,'shard_0'=16,'shard_1'=2,'shard_2'=2] {'shard_2'}, dimensions={0} | all-to-all | bytes 2097152 | tf_op jit(solution)/shard_map/all_to_all | solution.py:45
  360.5 1.0 stack.46
  361.6 15.3 %all-to-all-start.13 = ((bf16[16,2,16,4,128]{4,3,2,1,0:T(4,128)(2,1)}), bf16[16,2,16,4,128]{4,3,2,1,0:T(4,128)(2,1)}, u32[]{:S(2)}, u32[]{:S(2)}) async-start(bf16[16,2,16,4,128]{4,3,2,1,0:T(4,128)(2,1)} %stack.46), calls=%async_computation.13 | async-start | bytes 1048576 | tf_op jit(solution)/shard_map/all_to_all | solution.py:45
  376.9 1.5 copy.32
  378.4 1.6 copy.35
  380.0 1.4 fusion.3
  381.4 3.2 fusion
  384.6 2.2 copy.43
  386.7 2.5 copy.36
  389.2 3.1 reshape_reshape.15
  392.4 1.8 copy.39
  394.2 0.7 copy.40
  394.9 0.7 copy.41
  395.6 1.4 fusion.4
  397.0 1.4 fusion.5
  398.4 1.4 fusion.6
  399.8 2.9 all-to-all-done.13
  402.6 2.0 pad_maximum_fusion.3
  404.6 8.9 %all_to_all.108 = bf16[2,32,16,4,128]{4,3,2,1,0:T(4,128)(2,1)S(1)} all-to-all(bf16[2,32,16,4,128]{4,3,2,1,0:T(4,128)(2,1)S(1)} %pad_maximum_fusion.3), channel_id=1, replica_groups=mesh['grp'=8,'shard_0'=16,'shard_1'=2,'shard_2'=2] {'shard_2'}, dimensions={0} | all-to-all | bytes 2097152 | tf_op jit(solution)/shard_map/all_to_all | solution.py:45
  413.5 0.7 copy.42
  414.2 0.8 fusion.7
  415.2 0.8 maximum_multiply_fusion
  (38 shorter events, 0.5 us)
Async XLA Ops:
  0.6 379.4 %copy-start = (bf16[172,4096]{1,0:T(8,128)(2,1)S(1)}, bf16[172,4096]{1,0:T(8,128)(2,1)}, u32[]{:S(2)}) copy-start(bf16[172,4096]{1,0:T(8,128)(2,1)} %param.6) | copy-start | bytes 4227076
  28.6 8.2 %all-to-all-start.3 = ((bf16[2,1,16,4,128]{4,3,2,1,0:T(4,128)(2,1)}), bf16[2,1,16,4,128]{4,3,2,1,0:T(4,128)(2,1)S(1)}, u32[]{:S(2)}, u32[]{:S(2)}) async-start(bf16[2,1,16,4,128]{4,3,2,1,0:T(4,128)(2,1)} %pad_maximum_fusion.4), calls=%async_computation.3 | async-start | bytes 65536 | tf_op jit(solution)/shard_map/all_to_all | solution.py:45
  36.7 7.6 %all-to-all-start.6 = ((bf16[2,1,16,4,128]{4,3,2,1,0:T(4,128)(2,1)}), bf16[2,1,16,4,128]{4,3,2,1,0:T(4,128)(2,1)S(1)}, u32[]{:S(2)}, u32[]{:S(2)}) async-start(bf16[2,1,16,4,128]{4,3,2,1,0:T(4,128)(2,1)} %pad_maximum_fusion.5), calls=%async_computation.6 | async-start | bytes 65536 | tf_op jit(solution)/shard_map/all_to_all | solution.py:45
  44.3 7.6 %all-to-all-start.9 = ((bf16[2,1,16,4,128]{4,3,2,1,0:T(4,128)(2,1)}), bf16[2,1,16,4,128]{4,3,2,1,0:T(4,128)(2,1)S(1)}, u32[]{:S(2)}, u32[]{:S(2)}) async-start(bf16[2,1,16,4,128]{4,3,2,1,0:T(4,128)(2,1)} %pad_maximum_fusion.6), calls=%async_computation.9 | async-start | bytes 65536 | tf_op jit(solution)/shard_map/all_to_all | solution.py:45
  51.8 24.9 %all-to-all-start.12 = ((bf16[2,1,16,4,128]{4,3,2,1,0:T(4,128)(2,1)}), bf16[2,1,16,4,128]{4,3,2,1,0:T(4,128)(2,1)S(1)}, u32[]{:S(2)}, u32[]{:S(2)}) async-start(bf16[2,1,16,4,128]{4,3,2,1,0:T(4,128)(2,1)} %pad_maximum_fusion.7), calls=%async_computation.12 | async-start | bytes 65536 | tf_op jit(solution)/shard_map/all_to_all | solution.py:45
  76.7 110.8 %copy-start.13 = (bf16[2,1,16,4,128]{4,3,2,1,0:T(4,128)(2,1)}, bf16[2,1,16,4,128]{4,3,2,1,0:T(4,128)(2,1)S(1)}, u32[]{:S(2)}) copy-start(bf16[2,1,16,4,128]{4,3,2,1,0:T(4,128)(2,1)S(1)} %all-to-all-done.12) | copy-start | bytes 98308
  121.2 76.5 %copy-start.12 = (bf16[16,4096]{1,0:T(8,128)(2,1)S(1)}, bf16[16,4096]{1,0:T(8,128)(2,1)}, u32[]{:S(2)}) copy-start(bf16[16,4096]{1,0:T(8,128)(2,1)} %param.5) | copy-start | bytes 393220
  121.2 76.5 %copy-start.15 = (bf16[2,4,4096]{2,1,0:T(4,128)(2,1)S(1)}, bf16[2,4,4096]{2,1,0:T(4,128)(2,1)}, u32[]{:S(2)}) copy-start(bf16[2,4,4096]{2,1,0:T(4,128)(2,1)} %param.7) | copy-start | bytes 196612
  121.3 76.8 %copy-start.16 = (f32[2]{0:T(128)S(1)}, f32[2]{0:T(128)}, u32[]{:S(2)}) copy-start(f32[2]{0:T(128)} %param.9) | copy-start | bytes 28
  187.5 117.3 %all-to-all-start.10 = ((bf16[16,2,16,4,128]{4,3,2,1,0:T(4,128)(2,1)}), bf16[16,2,16,4,128]{4,3,2,1,0:T(4,128)(2,1)S(1)}, u32[]{:S(2)}, u32[]{:S(2)}) async-start(bf16[16,2,16,4,128]{4,3,2,1,0:T(4,128)(2,1)} %stack.43), calls=%async_computation.10 | async-start | bytes 1048576 | tf_op jit(solution)/shard_map/all_to_all | solution.py:45
  287.0 0.6 copy-start.8
  304.6 2.1 copy-start.7
  304.8 1.9 copy-start.5
  306.7 35.5 %all-to-all-start.1 = ((bf16[8,64,2,4,172]{4,3,2,1,0:T(4,128)(2,1)}), bf16[8,64,2,4,172]{4,3,2,1,0:T(4,128)(2,1)S(1)}, u32[]{:S(2)}, u32[]{:S(2)}) async-start(bf16[8,64,2,4,172]{4,3,2,1,0:T(4,128)(2,1)} %broadcast_in_dim.2), calls=%async_computation.1 | async-start | bytes 4194304 | tf_op jit(solution)/shard_map/all_to_all | solution.py:25
  311.9 6.0 %copy-start.6 = (bf16[16,2,16,4,128]{4,3,2,1,0:T(4,128)(2,1)S(1)}, bf16[16,2,16,4,128]{4,3,2,1,0:T(4,128)(2,1)}, u32[]{:S(2)}) copy-start(bf16[16,2,16,4,128]{4,3,2,1,0:T(4,128)(2,1)} %copy-done.5) | copy-start | bytes 1572868
  342.2 7.4 %copy-start.3 = (bf16[2,32,16,4,128]{4,3,2,1,0:T(4,128)(2,1)S(1)}, bf16[2,32,16,4,128]{4,3,2,1,0:T(4,128)(2,1)}, u32[]{:S(2)}) copy-start(bf16[2,32,16,4,128]{4,3,2,1,0:T(4,128)(2,1)} %pad_maximum_fusion.1) | copy-start | bytes 3145732
  342.2 12.9 %copy-start.4 = (bf16[2,32,16,4,128]{4,3,2,1,0:T(4,128)(2,1)S(1)}, bf16[2,32,16,4,128]{4,3,2,1,0:T(4,128)(2,1)}, u32[]{:S(2)}) copy-start(bf16[2,32,16,4,128]{4,3,2,1,0:T(4,128)(2,1)} %pad_maximum_fusion.2) | copy-start | bytes 3145732
  349.7 10.9 %copy-start.14 = (bf16[2,1,16,4,128]{4,3,2,1,0:T(4,128)(2,1)S(1)}, bf16[2,1,16,4,128]{4,3,2,1,0:T(4,128)(2,1)}, u32[]{:S(2)}) copy-start(bf16[2,1,16,4,128]{4,3,2,1,0:T(4,128)(2,1)} %copy-done.13) | copy-start | bytes 98308
  361.6 41.1 %all-to-all-start.13 = ((bf16[16,2,16,4,128]{4,3,2,1,0:T(4,128)(2,1)}), bf16[16,2,16,4,128]{4,3,2,1,0:T(4,128)(2,1)}, u32[]{:S(2)}, u32[]{:S(2)}) async-start(bf16[16,2,16,4,128]{4,3,2,1,0:T(4,128)(2,1)} %stack.46), calls=%async_computation.13 | async-start | bytes 1048576 | tf_op jit(solution)/shard_map/all_to_all | solution.py:45
  392.4 1.9 copy-start.1
  392.4 2.5 copy-start.2
  414.2 0.9 copy-start.9
  414.2 0.9 copy-start.10
  414.2 1.0 copy-start.11
